TPU v7x, 32 devices: a whole 2x2x4 slice. The times are simulated.
32 devices in a mesh: row: 4 (over x, core), col: 8 (over z, y).
Axes of the slice: x: 2, y: 2, z: 4, core: 2. Of those that a mesh axis runs over, the one named last changes fastest.
Arguments:
- tokens: bfloat16 [2048, 4096], P('col', 'row'), may hold values from -6 to 6
- gate_weight: bfloat16 [4096, 2048], P('row', 'col'), may hold values from -0.125 to 0.125
- up_weight: bfloat16 [4096, 2048], P('row', 'col'), may hold values from -0.125 to 0.125
- down_weight: bfloat16 [2048, 4096], P('col', 'row'), may hold values from -0.1875 to 0.1875
- gate_mask: int32 [16, 8], P('row', 'col'), may hold values from 0 to 1, as said below
- up_mask: int32 [16, 8], P('row', 'col'), may hold values from 0 to 1, as said below
- down_mask: int32 [8, 16], P('col', 'row'), may hold values from 0 to 1, as said below
Outputs:
- layer_out: bfloat16 [2048, 4096], P('col', 'row')
Inputs may be any that keep to these rules, and one draw needn't show every extreme that they name: `gate_mask`: every entry is 0 or 1; tile rows differ strongly in how many ones they hold, some rows nearly empty and some nearly full. `up_mask`: every entry is 0 or 1; tile rows differ strongly in how many ones they hold, some rows nearly empty and some nearly full. `down_mask`: every entry is 0 or 1; tile rows differ strongly in how many ones they hold, some rows nearly empty and some nearly full.
All inputs are finite; a program needn't handle non-finite values.
Results may differ from a plain program's by a relative error of at most 0.025.
Values may be sent and summed in bfloat16 or wider, within the bound.
A program may use at most 64 MiB of HBM per device.

v0:
```python
import jax
import jax.numpy as jnp
from jax import lax
from jax.sharding import PartitionSpec as P


def widen_mask(tile_mask, tile_size):
    return jnp.repeat(jnp.repeat(tile_mask, tile_size, axis=0), tile_size, axis=1).astype(
        jnp.bfloat16
    )


def prepare(weight, tile_mask):
    tile_size = weight.shape[0] // tile_mask.shape[0]
    return weight * widen_mask(tile_mask, tile_size)


def tile_product(rows_in, weight):
    return jnp.dot(rows_in, weight, preferred_element_type=jnp.float32)


def per_device(tokens, gate_weight, up_weight, down_weight, gate_mask, up_mask, down_mask):
    hidden_cols = gate_weight.shape[1]
    gate_ready = prepare(gate_weight, gate_mask)
    up_ready = prepare(up_weight, up_mask)
    down_ready = prepare(down_weight, down_mask)

    def project(rows_in):
        return jnp.concatenate(
            (tile_product(rows_in, gate_ready), tile_product(rows_in, up_ready)), axis=1
        )

    partial_sums = project(lax.all_gather(tokens, "col", axis=0, tiled=True))
    shares = lax.psum_scatter(
        partial_sums.astype(jnp.bfloat16), "row", scatter_dimension=0, tiled=True
    ).astype(jnp.float32)
    hidden_share = (jax.nn.silu(shares[:, :hidden_cols]) * shares[:, hidden_cols:]).astype(
        jnp.bfloat16
    )
    hidden = lax.all_gather(hidden_share, "row", axis=0, tiled=True)

    def output_term(row_count):
        rows_in = lax.slice_in_dim(hidden, 0, row_count, axis=0)
        return tile_product(rows_in, down_ready)

    layer_out = lax.psum_scatter(
        output_term(lax.axis_size("col") * tokens.shape[0]).astype(jnp.bfloat16),
        "col",
        scatter_dimension=0,
        tiled=True,
    ).astype(jnp.float32)
    return layer_out.astype(jnp.bfloat16)


def solution(mesh):
    return jax.shard_map(
        per_device,
        mesh=mesh,
        in_specs=(
            P("col", "row"),
            P("row", "col"),
            P("row", "col"),
            P("col", "row"),
            P("row", "col"),
            P("row", "col"),
            P("col", "row"),
        ),
        out_specs=P("col", "row"),
        check_vma=False,
    )
```

profile of v0, /device:TPU:0, one launch (start us, length us, event | category | flops | bytes accessed | tf_op | source)
XLA Modules:
  0.0 240.7 jit_solution(13478754110101655649)
XLA Ops:
  6.5 0.0 copy-start.2
  6.5 0.0 all-gather.3.cloned.1.call-start
  6.5 0.7 all-gather.3.cloned.1.call-update
  7.3 0.0 reduce-scatter.3.cloned.1.call-start
  7.3 0.7 convert_bitcast_fusion.2
  8.0 0.1 broadcast_bitcast_fusion.2
  8.0 0.7 convert_bitcast_fusion.1
  8.7 0.1 broadcast_bitcast_fusion.1
  8.8 76.6 %all-gather.3.cloned.1.call-done = bf16[2048,1024]{1,0:T(8,128)(2,1)} async-done(((bf16[256,1024]{1,0:T(8,128)(2,1)}), bf16[2048,1024]{1,0:T(8,128)(2,1)}) %all-gather.3.cloned.1.call-update) | async-done | bytes 4194320 | tf_op jit(solution)/shard_map/all_gather | solution.py:33
  85.4 0.0 copy-start.1
  85.4 4.0 %fusion = bf16[2048,256]{0,1:T(8,128)(2,1)S(1)} fusion(bf16[2048,1024]{1,0:T(8,128)(2,1)} %all-gather.3.cloned.1.call-done, bf16[1024,256]{1,0:T(8,128)(2,1)} %param.8, bf16[1024]{0:T(1024)(128)(2,1)S(1)} %bitcast.23), kind=kOutput, calls=%fused_computation.3 | convolution fusion | flops 1074528256 | bytes 5769216 | tf_op jit(solution)/shard_map/dot_general | solution.py:19
  89.4 0.0 copy-done.2
  89.4 0.0 copy-done.1
  89.4 1.6 fusion.1
  91.0 0.0 copy-start.3
  91.0 0.0 copy-start
  91.0 1.5 pad_maximum_fusion
  92.5 0.0 reduce-scatter.3.cloned.1.call-update
  92.5 0.0 all-gather.5.cloned.1.call-start
  92.6 29.3 %reduce-scatter.3.cloned.1.call-done = bf16[512,512]{0,1:T(8,128)(2,1)} async-done(((bf16[2048,512]{0,1:T(8,128)(2,1)}), bf16[512,512]{0,1:T(8,128)(2,1)}) %reduce-scatter.3.cloned.1.call-update) | async-done | bytes 524304 | tf_op jit(solution)/shard_map/reduce_scatter | solution.py:34
  121.9 1.2 convert_element_type.51
  123.0 0.9 fusion.2
  123.9 0.0 all-gather.5.cloned.1.call-update
  123.9 0.0 reduce-scatter.5.cloned.1.call-start
  124.0 0.0 copy-done.3
  124.0 0.1 broadcast_bitcast_fusion
  124.1 16.6 %all-gather.5.cloned.1.call-done = bf16[2048,256]{0,1:T(8,128)(2,1)} async-done(((bf16[512,256]{0,1:T(8,128)(2,1)}), bf16[2048,256]{0,1:T(8,128)(2,1)}) %all-gather.5.cloned.1.call-update) | async-done | bytes 1048592 | tf_op jit(solution)/shard_map/all_gather | solution.py:40
  140.7 0.0 copy-done
  140.7 4.5 %convolution_convert_fusion = bf16[2048,1024]{1,0:T(8,128)(2,1)} fusion(bf16[2048,256]{0,1:T(8,128)(2,1)} %all-gather.5.cloned.1.call-done, bf16[256,1024]{1,0:T(8,128)(2,1)S(1)} %copy-done, bf16[1024]{0:T(1024)(128)(2,1)S(1)} %bitcast.22), kind=kOutput, calls=%fused_computation | convolution fusion | flops 1076101120 | bytes 5769216 | tf_op jit(solution)/shard_map/dot_general | solution.py:19
  145.2 0.0 reduce-scatter.5.cloned.1.call-update
  145.2 89.0 %reduce-scatter.5.cloned.1.call-done = bf16[256,1024]{1,0:T(8,128)(2,1)} async-done(((bf16[2048,1024]{1,0:T(8,128)(2,1)}), bf16[256,1024]{1,0:T(8,128)(2,1)}) %reduce-scatter.5.cloned.1.call-update) | async-done | bytes 524304 | tf_op jit(solution)/shard_map/reduce_scatter | solution.py:46
  (4 shorter events, 0.0 us)
Async XLA Ops:
  6.5 82.9 %copy-start.2 = (bf16[1024,256]{1,0:T(8,128)(2,1)S(1)}, bf16[1024,256]{1,0:T(8,128)(2,1)}, u32[]{:S(2)}) copy-start(bf16[1024,256]{1,0:T(8,128)(2,1)} %param.9) | copy-start | bytes 1572868
  6.5 78.8 %all-gather.3.cloned.1.call-start = ((), (), s32[]{:S(2)}) async-start(), calls=%async_computation.2 | async-start | bytes 4718592 | tf_op jit(solution)/shard_map/all_gather | solution.py:33
  7.3 114.6 %reduce-scatter.3.cloned.1.call-start = ((), (), s32[]{:S(2)}) async-start(), calls=%async_computation.3 | async-start | bytes 2621440 | tf_op jit(solution)/shard_map/reduce_scatter | solution.py:34
  85.4 4.1 %copy-start.1 = (bf16[2048,1024]{1,0:T(8,128)(2,1)S(1)}, bf16[2048,1024]{1,0:T(8,128)(2,1)}, u32[]{:S(2)}) copy-start(bf16[2048,1024]{1,0:T(8,128)(2,1)} %all-gather.3.cloned.1.call-done) | copy-start | bytes 12582916
  91.0 33.0 %copy-start.3 = (s32[1,4]{1,0:T(1,128)S(1)}, s32[1,4]{1,0:T(1,128)}, u32[]{:S(2)}) copy-start(s32[1,4]{1,0:T(1,128)} %param.13) | copy-start | bytes 52
  91.0 49.7 %copy-start = (bf16[256,1024]{1,0:T(8,128)(2,1)S(1)}, bf16[256,1024]{1,0:T(8,128)(2,1)}, u32[]{:S(2)}) copy-start(bf16[256,1024]{1,0:T(8,128)(2,1)} %param.10) | copy-start | bytes 1572868
  92.5 48.2 %all-gather.5.cloned.1.call-start = ((), (), s32[]{:S(2)}) async-start(), calls=%async_computation.4 | async-start | bytes 1310720 | tf_op jit(solution)/shard_map/all_gather | solution.py:40
  123.9 110.2 %reduce-scatter.5.cloned.1.call-start = ((), (), s32[]{:S(2)}) async-start(), calls=%async_computation.5 | async-start | bytes 4718592 | tf_op jit(solution)/shard_map/reduce_scatter | solution.py:46
Sparse Core Ops, SparseCore 0:
  9.5 75.8 all-gather.2
  92.6 29.1 reduce-scatter.2
  124.0 16.5 all-gather.4
  145.3 88.8 reduce-scatter.4
where the time goes:
time: 241 us
  waiting for transfers between devices  212 us (88%)
  between operations  13.2 us (5%)
  matrix products  10.1 us (4%)
  other arithmetic  4.82 us (2%)
    reduce_scatter x1, waiting for transfers between devices, per_device(): lax.psum_scatter(output_term(lax.axis_size('col') * tokens.shape[0]).asty...  89 us
    all_gather x1, waiting for transfers between devices, per_device(): partial_sums = project(lax.all_gather(tokens, 'col', axis=0, tiled=True))  76.6 us
    reduce_scatter x1, waiting for transfers between devices, per_device(): lax.psum_scatter(partial_sums.astype(jnp.bfloat16), 'row', scatter_dimens...  29.3 us
    all_gather x1, waiting for transfers between devices, per_device(): hidden = lax.all_gather(hidden_share, 'row', axis=0, tiled=True)  16.6 us
    dot_general x3, matrix products, tile_product(): return jnp.dot(rows_in, weight, preferred_element_type=jnp.float32)  10.1 us
  transfers between devices with their start and end apart: 4, of which 4 were waited for; matrix products, arithmetic and copies ran while one was open for 1% of the time, Pallas kernels for 0%

commit v1 on v0

v1 whole, which is shorter than its diff:
```python
import functools

import jax
import jax.numpy as jnp
from jax import lax
from jax.experimental import pallas as pl
from jax.experimental.pallas import tpu as pltpu
from jax.sharding import PartitionSpec as P

MESH = pl.DeviceIdType.MESH
F32 = jnp.float32
BF16 = jnp.bfloat16
PAIR = 2
PIECES = 2


def pick(table, index):
    out = jnp.int32(table[0])
    for place, value in enumerate(table):
        if place:
            out = jnp.where(index == place, jnp.int32(value), out)
    return out


def arrival_orders(line):
    orders = []
    for a in range(line):
        orders.append(sorted(range(line), key=lambda b: (abs(b - a), b)))
    return orders


def reduce_orders(line):
    orders = []
    for a in range(line):
        orders.append(sorted((b for b in range(line) if b != a), key=lambda b: (-abs(b - a), b)))
    return orders


def kernel(
    line, xs,
    tok_hbm, gate_hbm, up_hbm, down_hbm, gmask, umask, dmask, out_hbm,
    xbuf, raw, rawd, w, wd, zsend, zrecv, zown, xsend, xrecv, hbuf, psend, pleft, pright, pown, obuf,
    loc, ag_r, ag_l, ag_in, wsem, cz_s, cz_r, xz_s, xz_r, xh_s, xh_r, ch_s, ch_r, p_s, pl_r, pr_r,
):
    row = lax.axis_index("row")
    col = lax.axis_index("col")
    core, x = row % 2, row // 2
    y, a = col % PAIR, col // PAIR
    tokens, k = tok_hbm.shape
    units = gate_hbm.shape[1]
    half = tokens // 2
    part = half // xs
    peer_core = {"row": x * 2 + 1 - core, "col": col}
    peer_y = {"row": row, "col": a * PAIR + 1 - y}
    right = {"row": row, "col": (a + 1) * PAIR + y}
    left = {"row": row, "col": (a - 1) * PAIR + y}
    has_right, has_left = a < line - 1, a > 0

    def at_x(d):
        return {"row": lax.rem(x + d, xs) * 2 + core, "col": col}

    def remote(src, dst, s, r, dev):
        return pltpu.make_async_remote_copy(
            src_ref=src, dst_ref=dst, send_sem=s, recv_sem=r, device_id=dev, device_id_type=MESH
        )

    loads = [
        pltpu.make_async_copy(tok_hbm, xbuf.at[a], loc.at[0]),
        pltpu.make_async_copy(gate_hbm, raw.at[0], loc.at[1]),
        pltpu.make_async_copy(up_hbm, raw.at[1], loc.at[2]),
        pltpu.make_async_copy(down_hbm, rawd, loc.at[3]),
    ]
    for c in loads:
        c.start()

    barrier = pltpu.get_barrier_semaphore()

    def greet(dev):
        pl.semaphore_signal(barrier, inc=1, device_id=dev, device_id_type=MESH)

    greet(peer_core)
    greet(peer_y)
    for d in range(1, xs):
        greet(at_x(d))

    @pl.when(has_right)
    def _():
        greet(right)

    @pl.when(has_left)
    def _():
        greet(left)

    ends = has_right.astype(jnp.int32) + has_left.astype(jnp.int32)
    pl.semaphore_wait(barrier, 1 + xs + ends)

    def go_right(b):
        return remote(xbuf.at[b], xbuf.at[b], ag_r.at[b], ag_in.at[b], right)

    def go_left(b):
        return remote(xbuf.at[b], xbuf.at[b], ag_l.at[b], ag_in.at[b], left)

    loads[0].wait()

    @pl.when(has_right)
    def _():
        go_right(a).start()

    @pl.when(has_left)
    def _():
        go_left(a).start()

    tile = k // gmask.shape[0]
    for which, mask in ((0, gmask), (1, umask)):
        loads[1 + which].wait()
        for i in range(mask.shape[0]):
            keep = mask[i, 0].astype(F32)
            rows = pl.ds(i * tile, tile)
            w[0, which, rows, :] = (raw[which, rows, :].astype(F32) * keep).astype(BF16)
    w_copy = remote(w.at[0], w.at[1], wsem.at[0], wsem.at[1], peer_y)
    w_copy.start()
    loads[3].wait()
    wide = down_hbm.shape[1] // dmask.shape[1]
    for i in range(dmask.shape[1]):
        keep = dmask[0, i].astype(F32)
        cols = pl.ds(i * wide, wide)
        wd[0, :, cols] = (rawd[:, cols].astype(F32) * keep).astype(BF16)
    d_copy = remote(wd.at[0], wd.at[1], wsem.at[2], wsem.at[3], peer_y)
    d_copy.start()

    arrive = arrival_orders(line)
    order = [pick([arrive[i][j] for i in range(line)], a) for j in range(line)]

    def take(j):
        b = order[j]
        go_right(b).wait_recv()

        @pl.when((b < a) & has_right)
        def _():
            go_right(b).start()

        @pl.when((b > a) & has_left)
        def _():
            go_left(b).start()

    def core_copy(s):
        return remote(zsend.at[s], zrecv.at[s], cz_s.at[s], cz_r.at[s], peer_core)

    def project(j, h):
        s = j * 2 + h
        b = order[j]

        def dots(rows):
            lhs = xbuf[b, rows, :]
            return [jnp.dot(lhs, w[h, i], preferred_element_type=F32) for i in range(2)]

        other = dots(pl.ds(pl.multiple_of((1 - core) * half, half), half))
        for i in range(2):
            zsend[s, i] = other[i].astype(BF16)
        core_copy(s).start()
        mine = dots(pl.ds(pl.multiple_of(core * half, half), half))
        for i in range(2):
            zown[s, i] = mine[i]

    def x_copy(s, d):
        to = lax.rem(x + d, xs)
        return remote(xsend.at[s, to], xrecv.at[s, d], xz_s.at[s, d], xz_r.at[s, d], at_x(d))

    def fold_core(s):
        core_copy(s).wait_recv()
        for i in range(2):
            total = zown[s, i] + zrecv[s, i].astype(F32)
            zown[s, i] = total
            for to in range(xs):
                xsend[s, to, i] = total[to * part:(to + 1) * part].astype(BF16)
        for d in range(1, xs):
            x_copy(s, d).start()

    def h_copy(s, d):
        return remote(hbuf.at[s, core, x], hbuf.at[s, core, x], xh_s.at[s, d], xh_r.at[s, d], at_x(d))

    def activate(s):
        rows = pl.ds(pl.multiple_of(x * part, part), part)
        acc = [zown[s, i, rows, :] for i in range(2)]
        for d in range(1, xs):
            x_copy(s, d).wait_recv()
            for i in range(2):
                acc[i] = acc[i] + xrecv[s, d, i].astype(F32)
        g, u = acc
        hbuf[s, core, x] = (g / (1.0 + jnp.exp(-g)) * u).astype(BF16)
        for d in range(1, xs):
            h_copy(s, d).start()

    def hc_copy(s):
        return remote(hbuf.at[s, core], hbuf.at[s, core], ch_s.at[s], ch_r.at[s], peer_core)

    def share(s):
        for d in range(1, xs):
            h_copy(s, d).wait_recv()
        hc_copy(s).start()

    def settle(s):
        hc_copy(s).wait_recv()

    def rest(group):
        for stage in (fold_core, activate, share, settle):
            for j, h in group:
                stage(j * 2 + h)

    middle = has_left & has_right
    first = [(j, 0) for j in range(line - 1)]
    second = [(j, 1) for j in range(line - 1)]
    third = [(line - 1, 0), (line - 1, 1)]
    for j, h in first:
        if j:
            take(j)
        project(j, h)
    rest(first)
    w_copy.wait_recv()
    for j, h in second:
        project(j, h)

    @pl.when(middle)
    def _():
        take(line - 1)

    rest(second)

    @pl.when(jnp.logical_not(middle))
    def _():
        take(line - 1)

    for j, h in third:
        project(j, h)
    rest(third)
    d_copy.wait_recv()

    size = tokens // PIECES
    far = reduce_orders(line)
    home = list(range(line))

    def term(j, q):
        acc = None
        for h in range(2):
            hid = hbuf[j * 2 + h].reshape(tokens, units)[q * size:(q + 1) * size]
            t = jnp.dot(hid, wd[h], preferred_element_type=F32)
            acc = t if acc is None else acc + t
        return acc

    def p_right(b, q):
        return remote(psend.at[b, q], pleft.at[b, q], p_s.at[b, q], pl_r.at[b, q], right)

    def p_left(b, q):
        return remote(psend.at[b, q], pright.at[b, q], p_s.at[b, q], pr_r.at[b, q], left)

    for j in range(line - 1, 0, -1):
        b = order[j]
        for q in range(PIECES):
            pown[...] = term(j, q)

            @pl.when((b > a) & has_left)
            def _():
                p_right(b, q).wait_recv()
                pown[...] += pleft[b, q].astype(F32)

            @pl.when((b < a) & has_right)
            def _():
                p_left(b, q).wait_recv()
                pown[...] += pright[b, q].astype(F32)

            psend[b, q] = pown[...].astype(BF16)

            @pl.when(b > a)
            def _():
                p_right(b, q).start()

            @pl.when(b < a)
            def _():
                p_left(b, q).start()

    for q in range(PIECES):
        pown[...] = term(0, q)

        @pl.when(has_left)
        def _():
            p_right(a, q).wait_recv()
            pown[...] += pleft[a, q].astype(F32)

        @pl.when(has_right)
        def _():
            p_left(a, q).wait_recv()
            pown[...] += pright[a, q].astype(F32)

        obuf[pl.ds(q * size, size), :] = pown[...].astype(BF16)
        pltpu.make_async_copy(
            obuf.at[pl.ds(q * size, size), :], out_hbm.at[pl.ds(q * size, size), :], loc.at[4 + q]
        ).start()

    w_copy.wait_send()
    d_copy.wait_send()
    for j in range(line):
        b = order[j]

        @pl.when((b <= a) & has_right)
        def _():
            go_right(b).wait_send()

        @pl.when((b >= a) & has_left)
        def _():
            go_left(b).wait_send()

        if j:
            for q in range(PIECES):
                p_right(b, q).wait_send()
        for h in range(2):
            s = j * 2 + h
            core_copy(s).wait_send()
            hc_copy(s).wait_send()
            for d in range(1, xs):
                x_copy(s, d).wait_send()
                h_copy(s, d).wait_send()
    for q in range(PIECES):
        pltpu.make_async_copy(
            obuf.at[pl.ds(q * size, size), :], out_hbm.at[pl.ds(q * size, size), :], loc.at[4 + q]
        ).wait()


def per_device(n_row, n_col, tokens, gate, up, down, gmask, umask, dmask):
    line, xs = n_col // PAIR, n_row // 2
    t, k = tokens.shape
    units = gate.shape[1]
    wide = down.shape[1]
    half = t // 2
    part = half // xs
    steps = 2 * line
    dma = pltpu.SemaphoreType.DMA
    vmem = pltpu.VMEM
    hbm = pl.BlockSpec(memory_space=pl.ANY)
    smem = pl.BlockSpec(memory_space=pltpu.SMEM)
    size = t // PIECES
    return pl.pallas_call(
        functools.partial(kernel, line, xs),
        out_shape=jax.ShapeDtypeStruct((t, wide), BF16),
        in_specs=[hbm] * 4 + [smem] * 3,
        out_specs=hbm,
        scratch_shapes=[
            vmem((line, t, k), BF16),
            vmem((2, k, units), BF16),
            vmem((units, wide), BF16),
            vmem((2, 2, k, units), BF16),
            vmem((2, units, wide), BF16),
            vmem((steps, 2, half, units), BF16),
            vmem((steps, 2, half, units), BF16),
            vmem((steps, 2, half, units), F32),
            vmem((steps, xs, 2, part, units), BF16),
            vmem((steps, xs, 2, part, units), BF16),
            vmem((steps, 2, xs, part, units), BF16),
            vmem((line, PIECES, size, wide), BF16),
            vmem((line, PIECES, size, wide), BF16),
            vmem((line, PIECES, size, wide), BF16),
            vmem((size, wide), F32),
            vmem((t, wide), BF16),
            dma((4 + PIECES,)),
            dma((line,)), dma((line,)), dma((line,)),
            dma((4,)),
            dma((steps,)), dma((steps,)),
            dma((steps, xs)), dma((steps, xs)),
            dma((steps, xs)), dma((steps, xs)),
            dma((steps,)), dma((steps,)),
            dma((line, PIECES)), dma((line, PIECES)), dma((line, PIECES)),
        ],
        compiler_params=pltpu.CompilerParams(
            collective_id=0, has_side_effects=True, vmem_limit_bytes=60 * 1024 * 1024
        ),
    )(tokens, gate, up, down, gmask, umask, dmask)


def solution(mesh):
    n_row, n_col = mesh.shape["row"], mesh.shape["col"]
    return jax.shard_map(
        functools.partial(per_device, n_row, n_col),
        mesh=mesh,
        in_specs=(
            P("col", "row"),
            P("row", "col"),
            P("row", "col"),
            P("col", "row"),
            P("row", "col"),
            P("row", "col"),
            P("col", "row"),
        ),
        out_specs=P("col", "row"),
        check_vma=False,
    )
```

time: 241 us -> 106 us (0.44)
  waiting for transfers between devices: 212 us -> 0 us
  Pallas kernels: 0 us -> 102 us
  between operations: 13.2 us -> 0.01 us
  matrix products: 10.1 us -> 0 us
  other arithmetic: 4.82 us -> 0 us
  local copies, waits for them, and re-layouts: 0.26 us -> 3.87 us
    reduce_scatter x2 -> x0, waiting for transfers between devices: 118 us -> none  [the longest x1 89 us: per_device(): lax.psum_scatter(output_term(lax.axis_size('col') * tokens.shape[0]).asty...]
    pallas_call x0 -> x1, Pallas kernels: none -> 102 us  [per_device(): pl.pallas_call(functools.partial(kernel, line, xs), out_shape=jax.ShapeDt...]
    all_gather x2 -> x0, waiting for transfers between devices: 93.2 us -> none  [the longest x1 76.6 us: per_device(): partial_sums = project(lax.all_gather(tokens, 'col', axis=0, tiled=True))]
    dot_general x3 -> x0, matrix products: 10.1 us -> none  [tile_product(): return jnp.dot(rows_in, weight, preferred_element_type=jnp.float32)]
    unnamed x14 -> x5, local copies, waits for them, and re-layouts: 0.26 us -> 3.87 us
    convert_element_type x5 -> x0, other arithmetic: 3.34 us -> none  [the longest x3 1.32 us: widen_mask(): jnp.repeat(jnp.repeat(tile_mask, tile_size, axis=0), tile_size, axis=1)]
  transfers between devices with their start and end apart: 4 -> 0, of which waited for: 4 -> 0; matrix products, arithmetic and copies ran while one was open for 1% -> 0% of each run, Pallas kernels for 0% -> 0%
where the time goes in v1:
time: 106 us
  Pallas kernels  102 us (96%)
  local copies, waits for them, and re-layouts  3.87 us (4%)
    pallas_call x1, Pallas kernels, per_device(): pl.pallas_call(functools.partial(kernel, line, xs), out_shape=jax.ShapeDt...  102 us
    unnamed x5, local copies, waits for them, and re-layouts  3.87 us

profile of v1, /device:TPU:0, one launch (start us, length us, event | category | flops | bytes accessed | tf_op | source)
XLA Modules:
  0.0 105.9 jit_solution(17711914448479110551)
XLA Ops:
  0.0 0.0 copy-start
  0.0 1.3 %copy.8.gmask = s32[4,1]{1,0:T(4,128)} copy(s32[4,1]{0,1:T(1,128)} %param.11) | data formatting | bytes 32 | tf_op args[4]
  1.3 0.0 copy-done
  1.3 0.7 copy.9.umask
  2.0 102.0 %shard_map.73 = bf16[256,1024]{1,0:T(8,128)(2,1)} custom-call(bf16[256,1024]{1,0:T(8,128)(2,1)} %tok_hbm.1, bf16[1024,256]{1,0:T(8,128)(2,1)} %gate_hbm.1, bf16[1024,256]{1,0:T(8,128)(2,1)} %up_hbm.1, bf16[256,1024]{1,0:T(8,128)(2,1)} %down_hbm.1, s32[4,1]{1,0:T(4,128)} %copy.8.gmask, s32[4,1]{1,0:T(4,128)} %copy.9.umask, s32[1,4]{1,0:T(1,128)} %dmask.1), custom_call_target="tpu_custom_call" | custom-call | tf_op jit(solution)/shard_map/pallas_call | solution.py:341
  104.0 1.9 %copy.11 = bf16[256,1024]{1,0:T(8,128)(2,1)} copy(bf16[256,1024]{1,0:T(8,128)(2,1)} %shard_map.73) | data formatting | bytes 1048576
Async XLA Ops:
  0.0 1.3 %copy-start = (s32[4,1]{0,1:T(1,128)S(1)}, s32[4,1]{0,1:T(1,128)}, u32[]{:S(2)}) copy-start(s32[4,1]{0,1:T(1,128)} %param.12) | copy-start | bytes 52

commit v2 on v1

--- a/solution.py
+++ b/solution.py
@@ -11,7 +11,8 @@
 F32 = jnp.float32
 BF16 = jnp.bfloat16
 PAIR = 2
-PIECES = 2
+PIECES = 4
+HALVES = 2
 
 
 def pick(table, index):
@@ -23,21 +24,23 @@
 
 
 def arrival_orders(line):
-    orders = []
-    for a in range(line):
-        orders.append(sorted(range(line), key=lambda b: (abs(b - a), b)))
-    return orders
+    return [sorted(range(line), key=lambda b: (abs(b - a), b)) for a in range(line)]
 
 
 def reduce_orders(line):
-    orders = []
-    for a in range(line):
-        orders.append(sorted((b for b in range(line) if b != a), key=lambda b: (-abs(b - a), b)))
-    return orders
+    sends = [line - 2, line - 1] + list(range(line - 3, 0, -1))
+    rank = {b: 2 * place for place, b in enumerate(sends)}
+
+    def key(a, b):
+        return rank[b] + a if b > a else rank[line - 1 - b] + line - 1 - a
+
+    return [
+        sorted((b for b in range(line) if b != a), key=lambda b: (key(a, b), b)) for a in range(line)
+    ]
 
 
 def kernel(
-    line, xs,
+    line, xs, tiles, down_tiles,
     tok_hbm, gate_hbm, up_hbm, down_hbm, gmask, umask, dmask, out_hbm,
     xbuf, raw, rawd, w, wd, zsend, zrecv, zown, xsend, xrecv, hbuf, psend, pleft, pright, pown, obuf,
     loc, ag_r, ag_l, ag_in, wsem, cz_s, cz_r, xz_s, xz_r, xh_s, xh_r, ch_s, ch_r, p_s, pl_r, pr_r,
@@ -46,9 +49,9 @@
     col = lax.axis_index("col")
     core, x = row % 2, row // 2
     y, a = col % PAIR, col // PAIR
-    tokens, k = tok_hbm.shape
+    _, half, k = tok_hbm.shape
+    tokens = 2 * half
     units = gate_hbm.shape[1]
-    half = tokens // 2
     part = half // xs
     peer_core = {"row": x * 2 + 1 - core, "col": col}
     peer_y = {"row": row, "col": a * PAIR + 1 - y}
@@ -94,54 +97,60 @@
     ends = has_right.astype(jnp.int32) + has_left.astype(jnp.int32)
     pl.semaphore_wait(barrier, 1 + xs + ends)
 
-    def go_right(b):
-        return remote(xbuf.at[b], xbuf.at[b], ag_r.at[b], ag_in.at[b], right)
-
-    def go_left(b):
-        return remote(xbuf.at[b], xbuf.at[b], ag_l.at[b], ag_in.at[b], left)
+    def go_right(b, q):
+        return remote(xbuf.at[b, q], xbuf.at[b, q], ag_r.at[b, q], ag_in.at[b, q], right)
+
+    def go_left(b, q):
+        return remote(xbuf.at[b, q], xbuf.at[b, q], ag_l.at[b, q], ag_in.at[b, q], left)
 
     loads[0].wait()
-
-    @pl.when(has_right)
-    def _():
-        go_right(a).start()
-
-    @pl.when(has_left)
-    def _():
-        go_left(a).start()
-
-    tile = k // gmask.shape[0]
+    for q in range(HALVES):
+
+        @pl.when(has_right)
+        def _():
+            go_right(a, q).start()
+
+        @pl.when(has_left)
+        def _():
+            go_left(a, q).start()
+
     for which, mask in ((0, gmask), (1, umask)):
         loads[1 + which].wait()
-        for i in range(mask.shape[0]):
-            keep = mask[i, 0].astype(F32)
-            rows = pl.ds(i * tile, tile)
-            w[0, which, rows, :] = (raw[which, rows, :].astype(F32) * keep).astype(BF16)
+        n_row, n_col = tiles
+        for i in range(n_row):
+            for j in range(n_col):
+                keep = mask[i * n_col + j].astype(F32)
+                rows = pl.ds(i * (k // n_row), k // n_row)
+                cols = pl.ds(j * (units // n_col), units // n_col)
+                w[0, which, rows, cols] = (raw[which, rows, cols].astype(F32) * keep).astype(BF16)
     w_copy = remote(w.at[0], w.at[1], wsem.at[0], wsem.at[1], peer_y)
     w_copy.start()
     loads[3].wait()
-    wide = down_hbm.shape[1] // dmask.shape[1]
-    for i in range(dmask.shape[1]):
-        keep = dmask[0, i].astype(F32)
-        cols = pl.ds(i * wide, wide)
-        wd[0, :, cols] = (rawd[:, cols].astype(F32) * keep).astype(BF16)
+    n_row, n_col = down_tiles
+    wide = down_hbm.shape[1]
+    for i in range(n_row):
+        for j in range(n_col):
+            keep = dmask[i * n_col + j].astype(F32)
+            rows = pl.ds(i * (units // n_row), units // n_row)
+            cols = pl.ds(j * (wide // n_col), wide // n_col)
+            wd[0, rows, cols] = (rawd[rows, cols].astype(F32) * keep).astype(BF16)
     d_copy = remote(wd.at[0], wd.at[1], wsem.at[2], wsem.at[3], peer_y)
     d_copy.start()
 
     arrive = arrival_orders(line)
     order = [pick([arrive[i][j] for i in range(line)], a) for j in range(line)]
 
-    def take(j):
+    def take(j, q):
         b = order[j]
-        go_right(b).wait_recv()
+        go_right(b, q).wait_recv()
 
         @pl.when((b < a) & has_right)
         def _():
-            go_right(b).start()
+            go_right(b, q).start()
 
         @pl.when((b > a) & has_left)
         def _():
-            go_left(b).start()
+            go_left(b, q).start()
 
     def core_copy(s):
         return remote(zsend.at[s], zrecv.at[s], cz_s.at[s], cz_r.at[s], peer_core)
@@ -150,15 +159,15 @@
         s = j * 2 + h
         b = order[j]
 
-        def dots(rows):
-            lhs = xbuf[b, rows, :]
+        def dots(which):
+            lhs = xbuf[b, which]
             return [jnp.dot(lhs, w[h, i], preferred_element_type=F32) for i in range(2)]
 
-        other = dots(pl.ds(pl.multiple_of((1 - core) * half, half), half))
+        other = dots(1 - core)
         for i in range(2):
             zsend[s, i] = other[i].astype(BF16)
         core_copy(s).start()
-        mine = dots(pl.ds(pl.multiple_of(core * half, half), half))
+        mine = dots(core)
         for i in range(2):
             zown[s, i] = mine[i]
 
@@ -208,36 +217,56 @@
                 stage(j * 2 + h)
 
     middle = has_left & has_right
-    first = [(j, 0) for j in range(line - 1)]
-    second = [(j, 1) for j in range(line - 1)]
-    third = [(line - 1, 0), (line - 1, 1)]
-    for j, h in first:
-        if j:
-            take(j)
-        project(j, h)
-    rest(first)
+    outer = jnp.logical_not(middle)
+    last = line - 1
+    second = [(j, 1) for j in range(last)]
+    third = [(last, 0), (last, 1)]
+
+    project(0, 0)
+    rest([(0, 0)])
+
+    @pl.when(middle)
+    def _():
+        for low in range(1, last, 2):
+            for q in range(HALVES):
+                for j in range(low, min(low + 2, last)):
+                    take(j, q)
+
+    for j in range(1, last):
+
+        @pl.when(outer)
+        def _():
+            for q in range(HALVES):
+                take(j, q)
+
+        project(j, 0)
+    rest([(j, 0) for j in range(1, last)])
+
+    @pl.when(middle)
+    def _():
+        for q in range(HALVES):
+            take(last, q)
+
     w_copy.wait_recv()
     for j, h in second:
         project(j, h)
 
     @pl.when(middle)
     def _():
-        take(line - 1)
-
-    rest(second)
-
-    @pl.when(jnp.logical_not(middle))
-    def _():
-        take(line - 1)
-
-    for j, h in third:
-        project(j, h)
-    rest(third)
+        for j, h in third:
+            project(j, h)
+        rest(second + third)
+
+    @pl.when(outer)
+    def _():
+        rest(second)
+
     d_copy.wait_recv()
 
     size = tokens // PIECES
     far = reduce_orders(line)
-    home = list(range(line))
+    targets = [pick([far[i][n] for i in range(line)], a) for n in range(last)]
+    spots = [pick([arrive[i].index(far[i][n]) for i in range(line)], a) for n in range(last)]
 
     def term(j, q):
         acc = None
@@ -253,10 +282,10 @@
     def p_left(b, q):
         return remote(psend.at[b, q], pright.at[b, q], p_s.at[b, q], pr_r.at[b, q], left)
 
-    for j in range(line - 1, 0, -1):
-        b = order[j]
+    def reduce(n):
+        b = targets[n]
         for q in range(PIECES):
-            pown[...] = term(j, q)
+            pown[...] = term(spots[n], q)
 
             @pl.when((b > a) & has_left)
             def _():
@@ -277,6 +306,19 @@
             @pl.when(b < a)
             def _():
                 p_left(b, q).start()
+
+    reduce(0)
+
+    @pl.when(outer)
+    def _():
+        for q in range(HALVES):
+            take(last, q)
+        for j, h in third:
+            project(j, h)
+        rest(third)
+
+    for n in range(1, last):
+        reduce(n)
 
     for q in range(PIECES):
         pown[...] = term(0, q)
@@ -301,13 +343,15 @@
     for j in range(line):
         b = order[j]
 
-        @pl.when((b <= a) & has_right)
-        def _():
-            go_right(b).wait_send()
-
-        @pl.when((b >= a) & has_left)
-        def _():
-            go_left(b).wait_send()
+        for q in range(HALVES):
+
+            @pl.when((b <= a) & has_right)
+            def _():
+                go_right(b, q).wait_send()
+
+            @pl.when((b >= a) & has_left)
+            def _():
+                go_left(b, q).wait_send()
 
         if j:
             for q in range(PIECES):
@@ -339,12 +383,12 @@
     smem = pl.BlockSpec(memory_space=pltpu.SMEM)
     size = t // PIECES
     return pl.pallas_call(
-        functools.partial(kernel, line, xs),
+        functools.partial(kernel, line, xs, gmask.shape, dmask.shape),
         out_shape=jax.ShapeDtypeStruct((t, wide), BF16),
         in_specs=[hbm] * 4 + [smem] * 3,
         out_specs=hbm,
         scratch_shapes=[
-            vmem((line, t, k), BF16),
+            vmem((line, HALVES, half, k), BF16),
             vmem((2, k, units), BF16),
             vmem((units, wide), BF16),
             vmem((2, 2, k, units), BF16),
@@ -361,7 +405,7 @@
             vmem((size, wide), F32),
             vmem((t, wide), BF16),
             dma((4 + PIECES,)),
-            dma((line,)), dma((line,)), dma((line,)),
+            dma((line, HALVES)), dma((line, HALVES)), dma((line, HALVES)),
             dma((4,)),
             dma((steps,)), dma((steps,)),
             dma((steps, xs)), dma((steps, xs)),
@@ -372,7 +416,7 @@
         compiler_params=pltpu.CompilerParams(
             collective_id=0, has_side_effects=True, vmem_limit_bytes=60 * 1024 * 1024
         ),
-    )(tokens, gate, up, down, gmask, umask, dmask)
+    )(tokens.reshape(HALVES, half, k), gate, up, down, *(m.reshape(-1) for m in (gmask, umask, dmask)))
 
 
 def solution(mesh):

time: 106 us -> 91.8 us (0.87)
  Pallas kernels: 102 us -> 89.8 us
  local copies, waits for them, and re-layouts: 3.87 us -> 1.87 us
    pallas_call x1, Pallas kernels: 102 us -> 89.8 us  [per_device(): pl.pallas_call(functools.partial(kernel, line, xs, gmask.shape, dmask.sha...]
    unnamed x5 -> x1, local copies, waits for them, and re-layouts: 3.87 us -> 1.87 us
where the time goes in v2:
time: 91.8 us; the launch traced here: 91.6 us
  Pallas kernels  89.8 us (98%)
  local copies, waits for them, and re-layouts  1.87 us (2%)
    pallas_call x1, Pallas kernels, per_device(): pl.pallas_call(functools.partial(kernel, line, xs, gmask.shape, dmask.sha...  89.8 us
    unnamed x1, local copies, waits for them, and re-layouts  1.87 us

profile of v2, /device:TPU:0, one launch (start us, length us, event | category | flops | bytes accessed | tf_op | source)
XLA Modules:
  0.0 91.6 jit_solution(7547354826159620612)
XLA Ops:
  0.0 89.8 %shard_map.73 = bf16[256,1024]{1,0:T(8,128)(2,1)} custom-call(bf16[2,128,1024]{2,1,0:T(8,128)(2,1)} %bitcast.4, bf16[1024,256]{1,0:T(8,128)(2,1)} %gate_hbm.1, bf16[1024,256]{1,0:T(8,128)(2,1)} %up_hbm.1, bf16[256,1024]{1,0:T(8,128)(2,1)} %down_hbm.1, s32[4]{0:T(128)} %bitcast.5, s32[4]{0:T(128)} %bitcast.6, s32[4]{0:T(128)} %bitcast.7), custom_call_target="tpu_custom_call" | custom-call | tf_op jit(solution)/shard_map/pallas_call | solution.py:385
  89.8 1.9 %copy.9 = bf16[256,1024]{1,0:T(8,128)(2,1)} copy(bf16[256,1024]{1,0:T(8,128)(2,1)} %shard_map.73) | data formatting | bytes 1048576

commit v3 on v2

--- a/solution.py
+++ b/solution.py
@@ -43,7 +43,7 @@
     line, xs, tiles, down_tiles,
     tok_hbm, gate_hbm, up_hbm, down_hbm, gmask, umask, dmask, out_hbm,
     xbuf, raw, rawd, w, wd, zsend, zrecv, zown, xsend, xrecv, hbuf, psend, pleft, pright, pown, obuf,
-    loc, ag_r, ag_l, ag_in, wsem, cz_s, cz_r, xz_s, xz_r, xh_s, xh_r, ch_s, ch_r, p_s, pl_r, pr_r,
+    loc, ag_r, ag_l, ag_in, wsem, d_s, d_r, cz_s, cz_r, xz_s, xz_r, xh_s, xh_r, ch_s, ch_r, p_s, pl_r, pr_r,
 ):
     row = lax.axis_index("row")
     col = lax.axis_index("col")
@@ -133,9 +133,15 @@
             keep = dmask[i * n_col + j].astype(F32)
             rows = pl.ds(i * (units // n_row), units // n_row)
             cols = pl.ds(j * (wide // n_col), wide // n_col)
-            wd[0, rows, cols] = (rawd[rows, cols].astype(F32) * keep).astype(BF16)
-    d_copy = remote(wd.at[0], wd.at[1], wsem.at[2], wsem.at[3], peer_y)
-    d_copy.start()
+            rawd[rows, cols] = (rawd[rows, cols].astype(F32) * keep).astype(BF16)
+    size = wide // PIECES
+    for q in range(PIECES):
+        wd[0, q] = rawd[:, q * size:(q + 1) * size]
+    def d_copy(q):
+        return remote(wd.at[0, q], wd.at[1, q], d_s.at[q], d_r.at[q], peer_y)
+
+    for q in range(PIECES):
+        d_copy(q).start()
 
     arrive = arrival_orders(line)
     order = [pick([arrive[i][j] for i in range(line)], a) for j in range(line)]
@@ -159,17 +165,14 @@
         s = j * 2 + h
         b = order[j]
 
-        def dots(which):
-            lhs = xbuf[b, which]
-            return [jnp.dot(lhs, w[h, i], preferred_element_type=F32) for i in range(2)]
-
-        other = dots(1 - core)
         for i in range(2):
-            zsend[s, i] = other[i].astype(BF16)
+            both = jnp.dot(
+                xbuf[b].reshape(tokens, k), w[h, i], preferred_element_type=F32
+            )
+            for q in range(HALVES):
+                zown[s, q, i] = both[q * half:(q + 1) * half]
+            zsend[s, i] = zown[s, 1 - core, i].astype(BF16)
         core_copy(s).start()
-        mine = dots(core)
-        for i in range(2):
-            zown[s, i] = mine[i]
 
     def x_copy(s, d):
         to = lax.rem(x + d, xs)
@@ -178,8 +181,8 @@
     def fold_core(s):
         core_copy(s).wait_recv()
         for i in range(2):
-            total = zown[s, i] + zrecv[s, i].astype(F32)
-            zown[s, i] = total
+            total = zown[s, core, i] + zrecv[s, i].astype(F32)
+            zown[s, core, i] = total
             for to in range(xs):
                 xsend[s, to, i] = total[to * part:(to + 1) * part].astype(BF16)
         for d in range(1, xs):
@@ -190,7 +193,7 @@
 
     def activate(s):
         rows = pl.ds(pl.multiple_of(x * part, part), part)
-        acc = [zown[s, i, rows, :] for i in range(2)]
+        acc = [zown[s, core, i, rows, :] for i in range(2)]
         for d in range(1, xs):
             x_copy(s, d).wait_recv()
             for i in range(2):
@@ -219,7 +222,7 @@
     middle = has_left & has_right
     outer = jnp.logical_not(middle)
     last = line - 1
-    second = [(j, 1) for j in range(last)]
+    second = [(j, 1) for j in range(last - 1, -1, -1)]
     third = [(last, 0), (last, 1)]
 
     project(0, 0)
@@ -247,6 +250,51 @@
         for q in range(HALVES):
             take(last, q)
 
+    far = reduce_orders(line)
+    targets = [pick([far[i][n] for i in range(line)], a) for n in range(last)]
+    spots = [pick([arrive[i].index(far[i][n]) for i in range(line)], a) for n in range(last)]
+
+    def term(j, q):
+        acc = None
+        for h in range(2):
+            hid = hbuf[j * 2 + h].reshape(tokens, units)
+            t = jnp.dot(hid, wd[h, q], preferred_element_type=F32)
+            acc = t if acc is None else acc + t
+        return acc
+
+    def p_right(b, q):
+        return remote(psend.at[b, q], pleft.at[b, q], p_s.at[b, q], pl_r.at[b, q], right)
+
+    def p_left(b, q):
+        return remote(psend.at[b, q], pright.at[b, q], p_s.at[b, q], pr_r.at[b, q], left)
+
+    def reduce(n):
+        b = targets[n]
+        for q in range(PIECES):
+            if n == 0:
+                d_copy(q).wait_recv()
+            pown[...] = term(spots[n], q)
+
+            @pl.when((b > a) & has_left)
+            def _():
+                p_right(b, q).wait_recv()
+                pown[...] += pleft[b, q].astype(F32)
+
+            @pl.when((b < a) & has_right)
+            def _():
+                p_left(b, q).wait_recv()
+                pown[...] += pright[b, q].astype(F32)
+
+            psend[b, q] = pown[...].astype(BF16)
+
+            @pl.when(b > a)
+            def _():
+                p_right(b, q).start()
+
+            @pl.when(b < a)
+            def _():
+                p_left(b, q).start()
+
     w_copy.wait_recv()
     for j, h in second:
         project(j, h)
@@ -256,65 +304,16 @@
         for j, h in third:
             project(j, h)
         rest(second + third)
+        reduce(0)
 
     @pl.when(outer)
     def _():
         rest(second)
-
-    d_copy.wait_recv()
-
-    size = tokens // PIECES
-    far = reduce_orders(line)
-    targets = [pick([far[i][n] for i in range(line)], a) for n in range(last)]
-    spots = [pick([arrive[i].index(far[i][n]) for i in range(line)], a) for n in range(last)]
-
-    def term(j, q):
-        acc = None
-        for h in range(2):
-            hid = hbuf[j * 2 + h].reshape(tokens, units)[q * size:(q + 1) * size]
-            t = jnp.dot(hid, wd[h], preferred_element_type=F32)
-            acc = t if acc is None else acc + t
-        return acc
-
-    def p_right(b, q):
-        return remote(psend.at[b, q], pleft.at[b, q], p_s.at[b, q], pl_r.at[b, q], right)
-
-    def p_left(b, q):
-        return remote(psend.at[b, q], pright.at[b, q], p_s.at[b, q], pr_r.at[b, q], left)
-
-    def reduce(n):
-        b = targets[n]
-        for q in range(PIECES):
-            pown[...] = term(spots[n], q)
-
-            @pl.when((b > a) & has_left)
-            def _():
-                p_right(b, q).wait_recv()
-                pown[...] += pleft[b, q].astype(F32)
-
-            @pl.when((b < a) & has_right)
-            def _():
-                p_left(b, q).wait_recv()
-                pown[...] += pright[b, q].astype(F32)
-
-            psend[b, q] = pown[...].astype(BF16)
-
-            @pl.when(b > a)
-            def _():
-                p_right(b, q).start()
-
-            @pl.when(b < a)
-            def _():
-                p_left(b, q).start()
-
-    reduce(0)
-
-    @pl.when(outer)
-    def _():
         for q in range(HALVES):
             take(last, q)
         for j, h in third:
             project(j, h)
+        reduce(0)
         rest(third)
 
     for n in range(1, last):
@@ -333,13 +332,14 @@
             p_left(a, q).wait_recv()
             pown[...] += pright[a, q].astype(F32)
 
-        obuf[pl.ds(q * size, size), :] = pown[...].astype(BF16)
+        obuf[:, pl.ds(q * size, size)] = pown[...].astype(BF16)
         pltpu.make_async_copy(
-            obuf.at[pl.ds(q * size, size), :], out_hbm.at[pl.ds(q * size, size), :], loc.at[4 + q]
+            obuf.at[:, pl.ds(q * size, size)], out_hbm.at[:, pl.ds(q * size, size)], loc.at[4 + q]
         ).start()
 
     w_copy.wait_send()
-    d_copy.wait_send()
+    for q in range(PIECES):
+        d_copy(q).wait_send()
     for j in range(line):
         b = order[j]
 
@@ -365,7 +365,7 @@
                 h_copy(s, d).wait_send()
     for q in range(PIECES):
         pltpu.make_async_copy(
-            obuf.at[pl.ds(q * size, size), :], out_hbm.at[pl.ds(q * size, size), :], loc.at[4 + q]
+            obuf.at[:, pl.ds(q * size, size)], out_hbm.at[:, pl.ds(q * size, size)], loc.at[4 + q]
         ).wait()
 
 
@@ -381,7 +381,7 @@
     vmem = pltpu.VMEM
     hbm = pl.BlockSpec(memory_space=pl.ANY)
     smem = pl.BlockSpec(memory_space=pltpu.SMEM)
-    size = t // PIECES
+    size = wide // PIECES
     return pl.pallas_call(
         functools.partial(kernel, line, xs, gmask.shape, dmask.shape),
         out_shape=jax.ShapeDtypeStruct((t, wide), BF16),
@@ -392,21 +392,21 @@
             vmem((2, k, units), BF16),
             vmem((units, wide), BF16),
             vmem((2, 2, k, units), BF16),
-            vmem((2, units, wide), BF16),
+            vmem((2, PIECES, units, size), BF16),
             vmem((steps, 2, half, units), BF16),
             vmem((steps, 2, half, units), BF16),
-            vmem((steps, 2, half, units), F32),
+            vmem((steps, HALVES, 2, half, units), F32),
             vmem((steps, xs, 2, part, units), BF16),
             vmem((steps, xs, 2, part, units), BF16),
             vmem((steps, 2, xs, part, units), BF16),
-            vmem((line, PIECES, size, wide), BF16),
-            vmem((line, PIECES, size, wide), BF16),
-            vmem((line, PIECES, size, wide), BF16),
-            vmem((size, wide), F32),
+            vmem((line, PIECES, t, size), BF16),
+            vmem((line, PIECES, t, size), BF16),
+            vmem((line, PIECES, t, size), BF16),
+            vmem((t, size), F32),
             vmem((t, wide), BF16),
             dma((4 + PIECES,)),
             dma((line, HALVES)), dma((line, HALVES)), dma((line, HALVES)),
-            dma((4,)),
+            dma((2,)), dma((PIECES,)), dma((PIECES,)),
             dma((steps,)), dma((steps,)),
             dma((steps, xs)), dma((steps, xs)),
             dma((steps, xs)), dma((steps, xs)),

time: 91.8 us -> 92.3 us (level)
  no operation moved by 1% of the time
where the time goes in v3:
time: 92.3 us; the launch traced here: 92.2 us
  Pallas kernels  90.3 us (98%)
  local copies, waits for them, and re-layouts  1.87 us (2%)
    pallas_call x1, Pallas kernels, per_device(): pl.pallas_call(functools.partial(kernel, line, xs, gmask.shape, dmask.sha...  90.3 us
    unnamed x1, local copies, waits for them, and re-layouts  1.87 us

profile of v3, /device:TPU:0, one launch (start us, length us, event | category | flops | bytes accessed | tf_op | source)
XLA Modules:
  0.0 92.2 jit_solution(6224107029046034947)
XLA Ops:
  0.0 90.3 %shard_map.73 = bf16[256,1024]{1,0:T(8,128)(2,1)} custom-call(bf16[2,128,1024]{2,1,0:T(8,128)(2,1)} %bitcast.4, bf16[1024,256]{1,0:T(8,128)(2,1)} %gate_hbm.1, bf16[1024,256]{1,0:T(8,128)(2,1)} %up_hbm.1, bf16[256,1024]{1,0:T(8,128)(2,1)} %down_hbm.1, s32[4]{0:T(128)} %bitcast.5, s32[4]{0:T(128)} %bitcast.6, s32[4]{0:T(128)} %bitcast.7), custom_call_target="tpu_custom_call" | custom-call | tf_op jit(solution)/shard_map/pallas_call | solution.py:385
  90.3 1.9 %copy.9 = bf16[256,1024]{1,0:T(8,128)(2,1)} copy(bf16[256,1024]{1,0:T(8,128)(2,1)} %shard_map.73) | data formatting | bytes 1048576

commit v4 on v3

--- a/solution.py
+++ b/solution.py
@@ -214,10 +214,13 @@
     def settle(s):
         hc_copy(s).wait_recv()
 
-    def rest(group):
-        for stage in (fold_core, activate, share, settle):
+    def run(stages, group):
+        for stage in stages:
             for j, h in group:
                 stage(j * 2 + h)
+
+    def rest(group):
+        run((fold_core, activate, share, settle), group)
 
     middle = has_left & has_right
     outer = jnp.logical_not(middle)
@@ -308,13 +311,15 @@
 
     @pl.when(outer)
     def _():
-        rest(second)
+        run((fold_core, activate), second)
         for q in range(HALVES):
             take(last, q)
         for j, h in third:
             project(j, h)
+        run((fold_core,), third)
+        run((share, settle), second)
         reduce(0)
-        rest(third)
+        run((activate, share, settle), third)
 
     for n in range(1, last):
         reduce(n)

time: 92.3 us -> 91.8 us (level)
  no operation moved by 1% of the time
where the time goes in v4:
time: 91.8 us; the launch traced here: 91.7 us
  Pallas kernels  89.8 us (98%)
  local copies, waits for them, and re-layouts  1.87 us (2%)
    pallas_call x1, Pallas kernels, per_device(): pl.pallas_call(functools.partial(kernel, line, xs, gmask.shape, dmask.sha...  89.8 us
    unnamed x1, local copies, waits for them, and re-layouts  1.87 us

profile of v4, /device:TPU:0, one launch (start us, length us, event | category | flops | bytes accessed | tf_op | source)
XLA Modules:
  0.0 91.7 jit_solution(9946095480334493571)
XLA Ops:
  0.0 89.8 %shard_map.73 = bf16[256,1024]{1,0:T(8,128)(2,1)} custom-call(bf16[2,128,1024]{2,1,0:T(8,128)(2,1)} %bitcast.4, bf16[1024,256]{1,0:T(8,128)(2,1)} %gate_hbm.1, bf16[1024,256]{1,0:T(8,128)(2,1)} %up_hbm.1, bf16[256,1024]{1,0:T(8,128)(2,1)} %down_hbm.1, s32[4]{0:T(128)} %bitcast.5, s32[4]{0:T(128)} %bitcast.6, s32[4]{0:T(128)} %bitcast.7), custom_call_target="tpu_custom_call" | custom-call | tf_op jit(solution)/shard_map/pallas_call | solution.py:390
  89.8 1.9 %copy.9 = bf16[256,1024]{1,0:T(8,128)(2,1)} copy(bf16[256,1024]{1,0:T(8,128)(2,1)} %shard_map.73) | data formatting | bytes 1048576
